TPU v7x, 32 devices: a whole 2x2x4 slice. The times are simulated.
32 devices in a mesh: dp: 16 (over z, y, core), mp: 2 (over x).
Axes of the slice: x: 2, y: 2, z: 4, core: 2. Of those that a mesh axis runs over, the one named last changes fastest.
Arguments:
- picture_tower_vectors: bfloat16 [3072, 1152], P('dp'), may hold values from -6 to 6
- caption_tower_vectors: bfloat16 [3072, 1152], P('dp', 'mp'), may hold values from -6 to 6
- picture_standardize_factor: float32 [1152], replicated, may hold values from 0.1 to 1.9
- picture_entry_matrix: bfloat16 [1152, 4304], P(None, 'mp'), may hold values from -0.1875 to 0.1875
- picture_exit_matrix: bfloat16 [4304, 1152], P('mp'), may hold values from -0.09375 to 0.09375
- caption_mapping_matrix: bfloat16 [1152, 1152], P('mp'), may hold values from -1 to 1
- energy_multiplier: float32 [], replicated, may hold values from 4 to 16
- energy_offset_term: float32 [], replicated, may hold values from -2 to -0.5
Outputs:
- grad_image: float32 [3072, 1152], P('dp', 'mp')
- grad_text: float32 [3072, 1152], P('dp', 'mp')
All inputs are finite; a program needn't handle non-finite values.
Results may differ from a plain program's by a relative error of at most 0.0046.
Values may be sent and summed in bfloat16 or wider, within the bound.
A program may use at most 64 MiB of HBM per device.

v0:
```python
import jax
import jax.numpy as jnp
from jax import lax
from jax.sharding import PartitionSpec as P


def gelu_tanh(values):
    return jax.nn.gelu(values, approximate=True)


def norm_back(upstream, unit_rows, inverse):
    unit_float = unit_rows.astype(jnp.float32)
    along = jnp.sum(unit_float * upstream, axis=-1, keepdims=True)
    return inverse * (upstream - unit_float * along)


def per_device(
    picture_tower_vectors,
    caption_tower_vectors,
    picture_standardize_factor,
    picture_entry_matrix,
    picture_exit_matrix,
    caption_mapping_matrix,
    energy_multiplier,
    energy_offset_term,
):
    rows_here = picture_tower_vectors.shape[0]
    width = picture_tower_vectors.shape[1]
    head_count = lax.axis_size("mp")
    head_pos = lax.axis_index("mp")
    cycle_size = lax.axis_size("dp")
    cycle_pos = lax.axis_index("dp")
    share = rows_here // head_count
    cols_here = caption_tower_vectors.shape[1]
    image_float = picture_tower_vectors.astype(jnp.float32)
    mean_row = jnp.mean(image_float, axis=-1, keepdims=True)
    variance = jnp.mean((image_float - mean_row) ** 2, axis=-1, keepdims=True)
    inv_std = lax.rsqrt(variance + 1e-06)
    centred = (image_float - mean_row) * inv_std
    normed = (centred * picture_standardize_factor).astype(jnp.bfloat16)
    preact = jnp.dot(normed, picture_entry_matrix, preferred_element_type=jnp.float32)
    hidden = gelu_tanh(preact).astype(jnp.bfloat16)
    partial_out = jnp.dot(hidden, picture_exit_matrix, preferred_element_type=jnp.float32)
    image_out = image_float + lax.psum(partial_out, "mp")
    inv_image = lax.rsqrt(jnp.sum(image_out * image_out, axis=-1, keepdims=True) + 1e-06)
    unit_image = (image_out * inv_image).astype(jnp.bfloat16)
    text_out = lax.psum_scatter(
        jnp.dot(caption_tower_vectors, caption_mapping_matrix, preferred_element_type=jnp.float32),
        "mp",
        scatter_dimension=0,
        tiled=True,
    )
    inv_text = lax.rsqrt(jnp.sum(text_out * text_out, axis=-1, keepdims=True) + 1e-06)
    unit_text = (text_out * inv_text).astype(jnp.bfloat16)
    image_ids = cycle_pos * rows_here + jnp.arange(rows_here, dtype=jnp.int32)
    piece = lax.all_gather(unit_text, "dp", axis=0, tiled=True)
    count = piece.shape[0]
    whole_pos = jnp.arange(count, dtype=jnp.int32)
    text_ids = whole_pos // share * rows_here + head_pos * share + whole_pos % share
    cosine_matrix = lax.dot_general(
        piece, unit_image, (((1,), (1,)), ((), ())), preferred_element_type=jnp.float32
    )
    couple_energies = energy_multiplier * cosine_matrix + energy_offset_term
    match_polarity = jnp.where(text_ids[:, None] == image_ids[None, :], 1.0, -1.0).astype(
        jnp.float32
    )
    polarity_scaled_energies = (
        energy_multiplier * -match_polarity * jax.nn.sigmoid(-match_polarity * couple_energies)
    ).astype(jnp.bfloat16)
    image_add = lax.dot_general(
        polarity_scaled_energies,
        piece,
        (((0,), (0,)), ((), ())),
        preferred_element_type=jnp.float32,
    )
    text_add = jnp.dot(polarity_scaled_energies, unit_image, preferred_element_type=jnp.float32)
    image_add, text_add = (image_add, text_add)
    text_store = text_add
    image_dir, text_store = (image_add, text_store)
    returned = lax.all_to_all(text_store, "dp", split_axis=0, concat_axis=0, tiled=True)
    text_dir = jnp.sum(returned.reshape(cycle_size, share, width), axis=0)
    image_total = lax.psum(image_dir, "mp")
    grad_out = norm_back(image_total, unit_image, inv_image)
    grad_out_b = grad_out.astype(jnp.bfloat16)
    grad_hidden = lax.dot_general(
        grad_out_b,
        picture_exit_matrix,
        (((1,), (1,)), ((), ())),
        preferred_element_type=jnp.float32,
    )
    unused, pull_back = jax.vjp(gelu_tanh, preact)
    grad_pre = pull_back(grad_hidden)[0].astype(jnp.bfloat16)
    partial_normed = lax.dot_general(
        grad_pre, picture_entry_matrix, (((1,), (1,)), ((), ())), preferred_element_type=jnp.float32
    )
    grad_normed = lax.psum_scatter(partial_normed, "mp", scatter_dimension=1, tiled=True)
    first_col = head_pos * cols_here
    gain_here = lax.dynamic_slice_in_dim(picture_standardize_factor, first_col, cols_here, 0)
    centred_here = lax.dynamic_slice_in_dim(centred, first_col, cols_here, 1)
    grad_out_here = lax.dynamic_slice_in_dim(grad_out, first_col, cols_here, 1)
    scaled = grad_normed * gain_here
    sum_one, sum_two = lax.psum(
        (jnp.sum(scaled, axis=-1), jnp.sum(scaled * centred_here, axis=-1)), "mp"
    )
    mean_one = (sum_one / width)[:, None]
    mean_two = (sum_two / width)[:, None]
    grad_image = grad_out_here + inv_std * (scaled - mean_one - centred_here * mean_two)
    grad_text_out = norm_back(text_dir, unit_text, inv_text).astype(jnp.bfloat16)
    grad_text = lax.dot_general(
        lax.all_gather(grad_text_out, "mp", axis=0, tiled=True),
        caption_mapping_matrix,
        (((1,), (1,)), ((), ())),
        preferred_element_type=jnp.float32,
    )
    return (grad_image, grad_text)


def solution(mesh):
    in_specs = (
        P("dp", None),
        P("dp", "mp"),
        P(),
        P(None, "mp"),
        P("mp", None),
        P("mp", None),
        P(),
        P(),
    )
    out_specs = (P("dp", "mp"), P("dp", "mp"))
    return jax.shard_map(
        per_device, mesh=mesh, in_specs=in_specs, out_specs=out_specs, check_vma=False
    )
```

profile of v0, /device:TPU:12, one launch (start us, length us, event | category | flops | bytes accessed | tf_op | source)
XLA Modules:
  0.0 306.5 jit_solution(9070903717060754251)
XLA Ops:
  7.2 0.0 copy-start
  7.2 0.0 copy-start.2
  7.2 0.0 copy-start.6
  7.2 0.0 reduce-scatter.5.cloned.1.call-start
  7.2 1.2 copy-done
  8.5 2.4 fusion.66
  10.9 0.0 reduce-scatter.5.cloned.1.call-update
  10.9 0.0 all-reduce.4.cloned.1.call-start
  11.0 0.0 copy-done.2
  11.0 0.1 convert_reduce_fusion
  11.1 0.0 slice-start
  11.2 0.3 fusion.17
  11.4 0.0 copy-done.6
  11.4 0.0 slice-start.1
  11.4 4.4 %fusion.37 = f32[192,2152]{1,0:T(8,128)S(1)} fusion(bf16[1152,2152]{0,1:T(8,128)(2,1)} %param.11, f32[1152]{0:T(1024)S(1)} %copy-done.6, bf16[192,1152]{1,0:T(8,128)(2,1)S(1)} %copy-done.2, f32[192]{0:T(256)S(1)} %add_rsqrt_fusion.1, f32[192]{0:T(256)S(1)} %broadcast_multiply_fusion.2), kind=kOutput, calls=%fused_computation.53 | convolution fusion | flops 953081856 | bytes 7059456 | tf_op jit(solution)/shard_map/dot_general | solution.py:41
  15.8 0.0 copy-start.7
  15.8 1.2 copy-done.7
  17.0 0.0 slice-done
  17.0 0.0 slice-done.1
  17.0 2.4 fusion.21
  19.4 0.0 all-reduce.4.cloned.1.call-update
  19.4 0.0 all-gather.2.cloned.1.call-start
  19.5 11.3 %reduce-scatter.5.cloned.1.call-done = f32[96,1152]{1,0:T(8,128)} async-done(((f32[192,1152]{1,0:T(8,128)}), f32[96,1152]{1,0:T(8,128)}) %reduce-scatter.5.cloned.1.call-update) | async-done | bytes 442384 | tf_op jit(solution)/shard_map/reduce_scatter | solution.py:47
  30.8 1.1 multiply_reduce_fusion.2
  31.9 1.8 multiply_convert_fusion.5
  33.7 0.0 all-gather.2.cloned.1.call-update
  35.1 34.5 %all-reduce.4.cloned.1.call-done = f32[192,1152]{1,0:T(8,128)} async-done(((f32[192,1152]{1,0:T(8,128)}), f32[192,1152]{1,0:T(8,128)}) %all-reduce.4.cloned.1.call-update) | async-done | bytes 884752 | tf_op jit(solution)/shard_map/psum | solution.py:44
  69.6 0.0 copy-start.5
  69.6 1.4 multiply_reduce_fusion
  71.1 0.0 copy-done.5
  71.1 0.3 fusion.15
  71.4 47.5 %all-gather.2.cloned.1.call-done = bf16[1536,1152]{1,0:T(8,128)(2,1)} async-done(((bf16[96,1152]{1,0:T(8,128)(2,1)}), bf16[1536,1152]{1,0:T(8,128)(2,1)}) %all-gather.2.cloned.1.call-update) | async-done | bytes 3538960 | tf_op jit(solution)/shard_map/all_gather | solution.py:56
  118.9 3.5 %fusion.7 = bf16[1536,192]{0,1:T(8,128)(2,1)S(1)} fusion(bf16[1536,1152]{1,0:T(8,128)(2,1)} %all-gather.2.cloned.1.call-done, bf16[192,1152]{1,0:T(8,128)(2,1)S(1)} %get-tuple-element.7, f32[]{:T(128)S(6)} %copy.15, s32[1536]{0:T(1024)S(1)} %fusion.53, f32[]{:T(128)S(6)} %copy.14, s32[192]{0:T(256)S(1)} %iota_add_fusion), kind=kOutput, calls=%fused_computation.9 | convolution fusion | flops 683016192 | bytes 4578056 | tf_op jit(solution)/shard_map/dot_general | solution.py:60
  122.4 0.0 copy-start.3
  122.4 4.2 %fusion.68 = f32[1536,1152]{1,0:T(8,128)} fusion(bf16[1536,192]{0,1:T(8,128)(2,1)S(1)} %fusion.7, bf16[192,1152]{1,0:T(8,128)(2,1)S(1)} %get-tuple-element.7), kind=kOutput, calls=%fused_computation.93 | convolution fusion | flops 679477248 | bytes 8110080 | tf_op jit(solution)/shard_map/dot_general | solution.py:76
  126.6 0.0 copy-done.3
  126.6 5.7 %all-to-all-start = ((f32[16,96,1152]{2,1,0:T(8,128)}), f32[16,96,1152]{2,1,0:T(8,128)}, u32[]{:S(2)}, u32[]{:S(2)}) async-start(f32[16,96,1152]{2,1,0:T(8,128)} %bitcast.18), calls=%async_computation.1 | async-start | bytes 14155776 | tf_op jit(solution)/shard_map/all_to_all | solution.py:80
  132.4 0.0 all-reduce.6.cloned.1.call-start
  132.4 4.1 %fusion.67 = f32[192,1152]{1,0:T(8,128)} fusion(bf16[1536,192]{0,1:T(8,128)(2,1)} %copy-done.3, bf16[1536,1152]{1,0:T(8,128)(2,1)} %all-gather.2.cloned.1.call-done), kind=kOutput, calls=%fused_computation.92 | convolution fusion | flops 679477248 | bytes 5013504 | tf_op jit(solution)/shard_map/dot_general | solution.py:70
  136.5 0.0 all-reduce.6.cloned.1.call-update
  136.5 0.0 reduce-scatter.7.cloned.1.call-start
  136.5 37.5 %all-reduce.6.cloned.1.call-done = f32[192,1152]{1,0:T(8,128)} async-done(((f32[192,1152]{1,0:T(8,128)}), f32[192,1152]{1,0:T(8,128)}) %all-reduce.6.cloned.1.call-update) | async-done | bytes 884752 | tf_op jit(solution)/shard_map/psum | solution.py:82
  174.1 0.0 copy-start.4
  174.1 1.4 fusion.18
  175.5 0.0 copy-done.4
  175.5 1.2 fusion.20
  176.7 9.4 %convolution_bitcast_fusion = f32[1152,192]{1,0:T(8,128)} fusion(bf16[1152,2152]{0,1:T(8,128)(2,1)} %param.11, f32[192,2152]{1,0:T(8,128)} %copy-done.7, bf16[2152,1152]{1,0:T(8,128)(2,1)} %param.12, f32[192,1152]{1,0:T(8,128)} %fusion.20), kind=kOutput, calls=%fused_computation | convolution fusion | flops 1912436736 | bytes 13338624
  186.0 0.0 reduce-scatter.7.cloned.1.call-update
  186.1 0.1 dynamic_slice.10
  186.2 21.9 %reduce-scatter.7.cloned.1.call-done = f32[576,192]{1,0:T(8,128)} async-done(((f32[1152,192]{1,0:T(8,128)}), f32[576,192]{1,0:T(8,128)}) %reduce-scatter.7.cloned.1.call-update) | async-done | bytes 442384
  208.1 1.3 copy.11
  209.3 0.3 multiply_reduce_fusion.3
  209.7 4.9 %all-reduce = (f32[192]{0:T(256)S(1)}, f32[192]{0:T(256)S(1)}) all-reduce(f32[192]{0:T(256)S(1)} %get-tuple-element.3, f32[192]{0:T(256)S(1)} %get-tuple-element.2), channel_id=1, replica_groups=mesh['dp'=16,'mp'=2] {'mp'}, use_global_device_ids=true, to_apply=%region_12.13 | all-reduce | flops 384 | bytes 3072 | tf_op jit(solution)/shard_map/psum | solution.py:102
  214.6 2.3 multiply_add_fusion
  216.9 0.0 copy-start.1
  216.9 69.5 %all-to-all-done = f32[16,96,1152]{2,1,0:T(8,128)} async-done(((f32[16,96,1152]{2,1,0:T(8,128)}), f32[16,96,1152]{2,1,0:T(8,128)}, u32[]{:S(2)}, u32[]{:S(2)}) %all-to-all-start) | async-done | bytes 7077920 | tf_op jit(solution)/shard_map/all_to_all | solution.py:80
  286.4 3.4 %reduce_sum.88 = f32[96,1152]{1,0:T(8,128)S(1)} reduce(f32[16,96,1152]{2,1,0:T(8,128)} %all-to-all-done, f32[]{:T(128)} %constant.19.clone.1), dimensions={0}, to_apply=%region_13.14 | reduce | flops 1658880 | bytes 7520260 | tf_op jit(solution)/shard_map/reduce_sum | solution.py:81
  289.7 0.0 copy-done.1
  289.8 0.2 fusion.33
  290.0 0.1 fusion.36
  290.1 8.4 %all_gather.7 = bf16[192,1152]{1,0:T(8,128)(2,1)S(1)} all-gather(bf16[96,1152]{1,0:T(8,128)(2,1)S(1)} %fusion.36), channel_id=1, replica_groups=mesh['dp'=16,'mp'=2] {'mp'}, dimensions={0}, use_global_device_ids=true | all-gather | bytes 663552 | tf_op jit(solution)/shard_map/all_gather | solution.py:110
  298.5 1.4 fusion.69
  (8 shorter events, 0.1 us)
Async XLA Ops:
  7.2 1.3 copy-start
  7.2 3.8 %copy-start.2 = (bf16[192,1152]{1,0:T(8,128)(2,1)S(1)}, bf16[192,1152]{1,0:T(8,128)(2,1)}, u32[]{:S(2)}) copy-start(bf16[192,1152]{1,0:T(8,128)(2,1)} %param.8) | copy-start | bytes 1327108
  7.2 4.2 %copy-start.6 = (f32[1152]{0:T(1024)S(1)}, f32[1152]{0:T(1024)}, u32[]{:S(2)}) copy-start(f32[1152]{0:T(1024)} %param.10) | copy-start | bytes 13828
  7.2 23.6 %reduce-scatter.5.cloned.1.call-start = ((), (), s32[]{:S(2)}) async-start(), calls=%async_computation.4 | async-start | bytes 1327104 | tf_op jit(solution)/shard_map/reduce_scatter | solution.py:47
  10.9 58.7 %all-reduce.4.cloned.1.call-start = ((), (), s32[]{:S(2)}) async-start(), calls=%async_computation.3 | async-start | bytes 1769472 | tf_op jit(solution)/shard_map/psum | solution.py:44
  11.1 5.9 %slice-start = ((s8[4958208]{0:T(1024)(128)(4,1)}), s8[4194304]{0:T(1024)(128)(4,1)S(1)}, s32[]{:S(2)}) async-start(s8[4958208]{0:T(1024)(128)(4,1)} %bitcast.20), calls=%async_computation.8 | async-start | bytes 8388608
  11.4 5.6 %slice-start.1 = ((s8[4958208]{0:T(1024)(128)(4,1)}), s8[763904]{0:T(1024)(128)(4,1)S(1)}, s32[]{:S(2)}) async-start(s8[4958208]{0:T(1024)(128)(4,1)} %bitcast.20), calls=%async_computation.9 | async-start | bytes 1527808
  15.8 1.2 copy-start.7
  19.4 99.5 %all-gather.2.cloned.1.call-start = ((), (), s32[]{:S(2)}) async-start(), calls=%async_computation.5 | async-start | bytes 3760128 | tf_op jit(solution)/shard_map/all_gather | solution.py:56
  69.6 1.5 copy-start.5
  122.4 4.2 %copy-start.3 = (bf16[1536,192]{0,1:T(8,128)(2,1)}, bf16[1536,192]{0,1:T(8,128)(2,1)S(1)}, u32[]{:S(2)}) copy-start(bf16[1536,192]{0,1:T(8,128)(2,1)S(1)} %fusion.7) | copy-start | bytes 1769476
  126.6 159.7 %all-to-all-start = ((f32[16,96,1152]{2,1,0:T(8,128)}), f32[16,96,1152]{2,1,0:T(8,128)}, u32[]{:S(2)}, u32[]{:S(2)}) async-start(f32[16,96,1152]{2,1,0:T(8,128)} %bitcast.18), calls=%async_computation.1 | async-start | bytes 14155776 | tf_op jit(solution)/shard_map/all_to_all | solution.py:80
  132.4 41.7 %all-reduce.6.cloned.1.call-start = ((), (), s32[]{:S(2)}) async-start(), calls=%async_computation.6 | async-start | bytes 1769472 | tf_op jit(solution)/shard_map/psum | solution.py:82
  136.5 71.6 %reduce-scatter.7.cloned.1.call-start = ((), (), s32[]{:S(2)}) async-start(), calls=%async_computation.7 | async-start | bytes 1769472
  174.1 1.4 copy-start.4
  216.9 72.9 %copy-start.1 = (f32[96,1152]{1,0:T(8,128)S(1)}, f32[96,1152]{1,0:T(8,128)}, u32[]{:S(2)}) copy-start(f32[96,1152]{1,0:T(8,128)} %reduce-scatter.5.cloned.1.call-done) | copy-start | bytes 1327108
Sparse Core Ops, SparseCore 0:
  11.1 19.6 reduce-scatter.4
  33.1 36.4 all-reduce.3
  72.5 46.3 all-gather.1
  136.6 37.4 all-reduce.5
  186.2 21.8 reduce-scatter.6
where the time goes:
time: 307 us; the launch traced here: 306 us
  waiting for transfers between devices  222 us (72%)
  matrix products  31.7 us (10%)
  between operations  15.3 us (5%)
  other arithmetic  14.1 us (5%)
  blocking collectives  13.3 us (4%)
  starting transfers between devices  5.93 us (2%)
  local copies, waits for them, and re-layouts  3.86 us (1%)
    all_to_all x1, waiting for transfers between devices, per_device(): lax.all_to_all(text_store, 'dp', split_axis=0, concat_axis=0, tiled=True)  69.5 us
    all_gather x1, waiting for transfers between devices, per_device(): piece = lax.all_gather(unit_text, 'dp', axis=0, tiled=True)  47.5 us
    psum x1, waiting for transfers between devices, per_device(): image_total = lax.psum(image_dir, 'mp')  37.5 us
    psum x1, waiting for transfers between devices, per_device(): image_out = image_float + lax.psum(partial_out, 'mp')  34.5 us
    unnamed x6, waiting for transfers between devices  22 us
    reduce_scatter x1, waiting for transfers between devices, per_device(): lax.psum_scatter(jnp.dot(caption_tower_vectors, caption_mapping_matrix, p...  11.3 us
    unnamed x1, matrix products  9.36 us
    all_gather x1, blocking collectives, per_device(): lax.all_gather(grad_text_out, 'mp', axis=0, tiled=True)  8.39 us
  transfers between devices with their start and end apart: 6, of which 6 were waited for; matrix products, arithmetic and copies ran while one was open for 10% of the time, Pallas kernels for 0%

commit v1 on v0

--- a/solution.py
+++ b/solution.py
@@ -53,7 +53,12 @@
     inv_text = lax.rsqrt(jnp.sum(text_out * text_out, axis=-1, keepdims=True) + 1e-06)
     unit_text = (text_out * inv_text).astype(jnp.bfloat16)
     image_ids = cycle_pos * rows_here + jnp.arange(rows_here, dtype=jnp.int32)
-    piece = lax.all_gather(unit_text, "dp", axis=0, tiled=True)
+    ring = [unit_text]
+    for hop in range(15):
+        ring.append(lax.ppermute(ring[-1], "dp", [(dev, (dev + 1) % 16) for dev in range(16)]))
+    piece = jnp.roll(
+        jnp.concatenate(ring[::-1], axis=0), (lax.axis_index("dp") + 1) * ring[0].shape[0], axis=0
+    )
     count = piece.shape[0]
     whole_pos = jnp.arange(count, dtype=jnp.int32)
     text_ids = whole_pos // share * rows_here + head_pos * share + whole_pos % share

time: 307 us -> 356 us (1.16)
  starting transfers between devices: 5.93 us -> 41.7 us
  local copies, waits for them, and re-layouts: 3.86 us -> 17.6 us
  other arithmetic: 14.1 us -> 19.4 us
  waiting for transfers between devices: 222 us -> 217 us
    all_gather x1 -> x0, waiting for transfers between devices: 47.5 us -> none  [per_device(): piece = lax.all_gather(unit_text, 'dp', axis=0, tiled=True)]
    ppermute x0 -> x15, waiting for transfers between devices: none -> 41.5 us  [per_device(): lax.ppermute(ring[-1], 'dp', [(dev, (dev + 1) % 16) for dev in range(16)])]
    ppermute x0 -> x15, starting transfers between devices: none -> 31 us  [per_device(): lax.ppermute(ring[-1], 'dp', [(dev, (dev + 1) % 16) for dev in range(16)])]
    unnamed x21 -> x105, local copies, waits for them, and re-layouts: 3.78 us -> 17.5 us
    reduce_scatter x1, waiting for transfers between devices: 11.3 us -> 19.8 us  [per_device(): lax.psum_scatter(jnp.dot(caption_tower_vectors, caption_mapping_matrix, p...]
    psum x1, waiting for transfers between devices: 34.5 us -> 28.7 us  [per_device(): image_out = image_float + lax.psum(partial_out, 'mp')]
    all_to_all x1, starting transfers between devices: 5.72 us -> 10.4 us  [per_device(): lax.all_to_all(text_store, 'dp', split_axis=0, concat_axis=0, tiled=True)]
    unnamed x6 -> x5, waiting for transfers between devices: 22 us -> 21.9 us
  transfers between devices with their start and end apart: 6 -> 20, of which waited for: 6 -> 17; matrix products, arithmetic and copies ran while one was open for 10% -> 10% of each run, Pallas kernels for 0% -> 0%
where the time goes in v1:
time: 356 us; the launch traced here: 355 us
  waiting for transfers between devices  217 us (61%)
  starting transfers between devices  41.7 us (12%)
  matrix products  30.2 us (8%)
  other arithmetic  19.4 us (5%)
  local copies, waits for them, and re-layouts  17.6 us (5%)
  between operations  15.7 us (4%)
  blocking collectives  13.3 us (4%)
    all_to_all x1, waiting for transfers between devices, per_device(): lax.all_to_all(text_store, 'dp', split_axis=0, concat_axis=0, tiled=True)  69 us
    ppermute x15, waiting for transfers between devices, per_device(): lax.ppermute(ring[-1], 'dp', [(dev, (dev + 1) % 16) for dev in range(16)])  41.5 us
    psum x1, waiting for transfers between devices, per_device(): image_total = lax.psum(image_dir, 'mp')  36.5 us
    ppermute x15, starting transfers between devices, per_device(): lax.ppermute(ring[-1], 'dp', [(dev, (dev + 1) % 16) for dev in range(16)])  31 us
    psum x1, waiting for transfers between devices, per_device(): image_out = image_float + lax.psum(partial_out, 'mp')  28.7 us
    unnamed x5, waiting for transfers between devices  21.9 us
    reduce_scatter x1, waiting for transfers between devices, per_device(): lax.psum_scatter(jnp.dot(caption_tower_vectors, caption_mapping_matrix, p...  19.8 us
    unnamed x105, local copies, waits for them, and re-layouts  17.5 us
  transfers between devices with their start and end apart: 20, of which 17 were waited for; matrix products, arithmetic and copies ran while one was open for 10% of the time, Pallas kernels for 0%

profile of v1, /device:TPU:12, one launch (start us, length us, event | category | flops | bytes accessed | tf_op | source)
XLA Modules:
  0.0 355.3 jit_solution(8140189280361972000)
XLA Ops:
  7.2 1.3 copy-done
  8.5 2.4 fusion.91
  11.0 19.8 %reduce-scatter.5.cloned.1.call-done = f32[96,1152]{1,0:T(8,128)} async-done(((f32[192,1152]{1,0:T(8,128)}), f32[96,1152]{1,0:T(8,128)}) %reduce-scatter.5.cloned.1.call-update) | async-done | bytes 442384 | tf_op jit(solution)/shard_map/reduce_scatter | solution.py:47
  30.8 1.3 multiply_reduce_fusion.2
  32.1 1.2 multiply_convert_fusion.5
  33.4 5.3 %collective-permute-done = bf16[96,1152]{1,0:T(8,128)(2,1)S(1)} collective-permute-done((bf16[96,1152]{1,0:T(8,128)(2,1)S(1)}, bf16[96,1152]{1,0:T(8,128)(2,1)S(1)}, u32[]{:S(2)}, u32[]{:S(2)}) %collective-permute-start) | collective-permute-done | bytes 221216 | tf_op jit(solution)/shard_map/ppermute | solution.py:58
  38.7 5.4 %collective-permute-done.1 = bf16[96,1152]{1,0:T(8,128)(2,1)S(1)} collective-permute-done((bf16[96,1152]{1,0:T(8,128)(2,1)S(1)}, bf16[96,1152]{1,0:T(8,128)(2,1)S(1)}, u32[]{:S(2)}, u32[]{:S(2)}) %collective-permute-start.1) | collective-permute-done | bytes 221216 | tf_op jit(solution)/shard_map/ppermute | solution.py:58
  44.1 5.4 %collective-permute-done.2 = bf16[96,1152]{1,0:T(8,128)(2,1)S(1)} collective-permute-done((bf16[96,1152]{1,0:T(8,128)(2,1)S(1)}, bf16[96,1152]{1,0:T(8,128)(2,1)S(1)}, u32[]{:S(2)}, u32[]{:S(2)}) %collective-permute-start.2) | collective-permute-done | bytes 221216 | tf_op jit(solution)/shard_map/ppermute | solution.py:58
  50.1 0.9 collective-permute-start.3
  51.0 4.5 %collective-permute-done.3 = bf16[96,1152]{1,0:T(8,128)(2,1)S(1)} collective-permute-done((bf16[96,1152]{1,0:T(8,128)(2,1)S(1)}, bf16[96,1152]{1,0:T(8,128)(2,1)S(1)}, u32[]{:S(2)}, u32[]{:S(2)}) %collective-permute-start.3) | collective-permute-done | bytes 221216 | tf_op jit(solution)/shard_map/ppermute | solution.py:58
  55.5 0.7 copy-done.11
  56.2 1.8 collective-permute-start.4
  58.0 1.2 convert_reduce_fusion
  59.1 2.4 collective-permute-done.4
  61.5 0.7 copy-done.13
  62.2 2.7 collective-permute-start.5
  64.9 1.3 fusion.40
  66.2 1.4 collective-permute-done.5
  68.3 3.6 %collective-permute-start.6 = (bf16[96,1152]{1,0:T(8,128)(2,1)S(1)}, bf16[96,1152]{1,0:T(8,128)(2,1)S(1)}, u32[]{:S(2)}, u32[]{:S(2)}) collective-permute-start(bf16[96,1152]{1,0:T(8,128)(2,1)S(1)} %collective-permute-done.5), channel_id=1, source_target_pairs={{0,2},{2,4},{4,6},{6,8},{8,10},{10,12},{12,14},{14,16},{16,18},{18... | collective-permute-start | bytes 663560 | tf_op jit(solution)/shard_map/ppermute | solution.py:58
  71.9 1.8 collective-permute-done.6
  73.7 4.5 %collective-permute-start.7 = (bf16[96,1152]{1,0:T(8,128)(2,1)S(1)}, bf16[96,1152]{1,0:T(8,128)(2,1)S(1)}, u32[]{:S(2)}, u32[]{:S(2)}) collective-permute-start(bf16[96,1152]{1,0:T(8,128)(2,1)S(1)} %collective-permute-done.6), channel_id=1, source_target_pairs={{0,2},{2,4},{4,6},{6,8},{8,10},{10,12},{12,14},{14,16},{16,18},{18... | collective-permute-start | bytes 663560 | tf_op jit(solution)/shard_map/ppermute | solution.py:58
  78.2 4.4 %fusion.60 = f32[192,2152]{1,0:T(8,128)S(1)} fusion(bf16[1152,2152]{0,1:T(8,128)(2,1)} %param.11, f32[1152]{0:T(1024)} %param.10, bf16[192,1152]{1,0:T(8,128)(2,1)} %param.8, f32[192]{0:T(256)S(1)} %add_rsqrt_fusion.1, f32[192]{0:T(256)S(1)} %broadcast_multiply_fusion.2), kind=kOutput, calls=%fused_computation.57 | convolution fusion | flops 953081856 | bytes 7059456 | tf_op jit(solution)/shard_map/dot_general | solution.py:41
  82.6 3.4 collective-permute-start.8
  86.0 2.4 fusion.44
  88.5 2.2 collective-permute-start.9
  90.7 3.3 collective-permute-done.9
  93.9 3.0 collective-permute-start.10
  96.9 2.4 collective-permute-done.10
  99.3 3.9 %collective-permute-start.11 = (bf16[96,1152]{1,0:T(8,128)(2,1)S(1)}, bf16[96,1152]{1,0:T(8,128)(2,1)S(1)}, u32[]{:S(2)}, u32[]{:S(2)}) collective-permute-start(bf16[96,1152]{1,0:T(8,128)(2,1)S(1)} %collective-permute-done.10), channel_id=1, source_target_pairs={{0,2},{2,4},{4,6},{6,8},{8,10},{10,12},{12,14},{14,16},{16,18},{18... | collective-permute-start | bytes 663560 | tf_op jit(solution)/shard_map/ppermute | solution.py:58
  103.8 0.9 collective-permute-done.11
  104.6 4.8 %collective-permute-start.12 = (bf16[96,1152]{1,0:T(8,128)(2,1)S(1)}, bf16[96,1152]{1,0:T(8,128)(2,1)S(1)}, u32[]{:S(2)}, u32[]{:S(2)}) collective-permute-start(bf16[96,1152]{1,0:T(8,128)(2,1)S(1)} %collective-permute-done.11), channel_id=1, source_target_pairs={{0,2},{2,4},{4,6},{6,8},{8,10},{10,12},{12,14},{14,16},{16,18},{18... | collective-permute-start | bytes 663560 | tf_op jit(solution)/shard_map/ppermute | solution.py:58
  111.3 28.7 %all-reduce.4.cloned.1.call-done = f32[192,1152]{1,0:T(8,128)} async-done(((f32[192,1152]{1,0:T(8,128)}), f32[192,1152]{1,0:T(8,128)}) %all-reduce.4.cloned.1.call-update) | async-done | bytes 884752 | tf_op jit(solution)/shard_map/psum | solution.py:44
  140.0 1.4 multiply_reduce_fusion
  141.6 5.3 %collective-permute-done.13 = bf16[96,1152]{1,0:T(8,128)(2,1)S(1)} collective-permute-done((bf16[96,1152]{1,0:T(8,128)(2,1)S(1)}, bf16[96,1152]{1,0:T(8,128)(2,1)S(1)}, u32[]{:S(2)}, u32[]{:S(2)}) %collective-permute-start.13) | collective-permute-done | bytes 221216 | tf_op jit(solution)/shard_map/ppermute | solution.py:58
  147.1 1.6 fusion.38
  148.7 3.7 %collective-permute-done.14 = bf16[96,1152]{1,0:T(8,128)(2,1)S(1)} collective-permute-done((bf16[96,1152]{1,0:T(8,128)(2,1)S(1)}, bf16[96,1152]{1,0:T(8,128)(2,1)S(1)}, u32[]{:S(2)}, u32[]{:S(2)}) %collective-permute-start.14) | collective-permute-done | bytes 221216 | tf_op jit(solution)/shard_map/ppermute | solution.py:58
  152.4 1.0 constant_dynamic-update-slice_fusion.29
  153.4 1.0 constant_dynamic-update-slice_fusion.28
  154.4 1.0 constant_dynamic-update-slice_fusion.27
  155.3 1.0 constant_dynamic-update-slice_fusion.26
  156.3 1.0 constant_dynamic-update-slice_fusion.25
  157.2 1.0 constant_dynamic-update-slice_fusion.24
  158.2 1.0 constant_dynamic-update-slice_fusion.22
  159.2 1.0 constant_dynamic-update-slice_fusion.21
  160.2 1.0 constant_dynamic-update-slice_fusion.20
  161.1 1.0 constant_dynamic-update-slice_fusion.19
  163.0 1.7 fusion.28
  164.7 1.1 copy-done.4
  165.8 0.8 copy-done.3
  166.6 4.2 %fusion.92 = f32[1536,1152]{1,0:T(8,128)} fusion(bf16[1536,192]{0,1:T(8,128)(2,1)S(1)} %fusion.28, bf16[192,1152]{1,0:T(8,128)(2,1)S(1)} %get-tuple-element.7), kind=kOutput, calls=%fused_computation.130 | convolution fusion | flops 679477248 | bytes 8110080 | tf_op jit(solution)/shard_map/dot_general | solution.py:81
  170.8 10.4 %all-to-all-start = ((f32[16,96,1152]{2,1,0:T(8,128)}), f32[16,96,1152]{2,1,0:T(8,128)}, u32[]{:S(2)}, u32[]{:S(2)}) async-start(f32[16,96,1152]{2,1,0:T(8,128)} %bitcast.16), calls=%async_computation.1 | async-start | bytes 14155776 | tf_op jit(solution)/shard_map/all_to_all | solution.py:85
  181.2 4.3 %fusion = f32[192,1152]{1,0:T(8,128)} fusion(bf16[1536,192]{0,1:T(8,128)(2,1)} %copy-done.3, bf16[3072,1152]{1,0:T(8,128)(2,1)} %copy-done.4, s32[]{:T(128)S(6)} %select_n.45), kind=kOutput, calls=%fused_computation | convolution fusion | flops 679477248 | bytes 5013508 | tf_op jit(solution)/shard_map/dot_general | solution.py:75
  185.8 36.5 %all-reduce.6.cloned.1.call-done = f32[192,1152]{1,0:T(8,128)} async-done(((f32[192,1152]{1,0:T(8,128)}), f32[192,1152]{1,0:T(8,128)}) %all-reduce.6.cloned.1.call-update) | async-done | bytes 884752 | tf_op jit(solution)/shard_map/psum | solution.py:87
  222.3 1.3 fusion.41
  223.6 2.4 fusion.43
  226.0 9.4 %convolution_bitcast_fusion = f32[1152,192]{1,0:T(8,128)} fusion(bf16[1152,2152]{0,1:T(8,128)(2,1)} %param.11, f32[192,2152]{1,0:T(8,128)} %copy-done.34, bf16[2152,1152]{1,0:T(8,128)(2,1)} %param.12, f32[192,1152]{1,0:T(8,128)} %fusion.43), kind=kOutput, calls=%fused_computation.4 | convolution fusion | flops 1912436736 | bytes 13338624
  235.5 21.9 %reduce-scatter.7.cloned.1.call-done = f32[576,192]{1,0:T(8,128)} async-done(((f32[1152,192]{1,0:T(8,128)}), f32[576,192]{1,0:T(8,128)}) %reduce-scatter.7.cloned.1.call-update) | async-done | bytes 442384
  257.4 1.3 copy.11
  259.0 4.9 %all-reduce = (f32[192]{0:T(256)S(1)}, f32[192]{0:T(256)S(1)}) all-reduce(f32[192]{0:T(256)S(1)} %get-tuple-element.3, f32[192]{0:T(256)S(1)} %get-tuple-element.2), channel_id=1, replica_groups=mesh['dp'=16,'mp'=2] {'mp'}, use_global_device_ids=true, to_apply=%region_12.13 | all-reduce | flops 384 | bytes 3072 | tf_op jit(solution)/shard_map/psum | solution.py:107
  263.9 2.3 multiply_add_fusion
  266.2 69.0 %all-to-all-done = f32[16,96,1152]{2,1,0:T(8,128)} async-done(((f32[16,96,1152]{2,1,0:T(8,128)}), f32[16,96,1152]{2,1,0:T(8,128)}, u32[]{:S(2)}, u32[]{:S(2)}) %all-to-all-start) | async-done | bytes 7077920 | tf_op jit(solution)/shard_map/all_to_all | solution.py:85
  335.2 3.4 reduce_sum.88
  338.9 8.4 %all_gather.3 = bf16[192,1152]{1,0:T(8,128)(2,1)S(1)} all-gather(bf16[96,1152]{1,0:T(8,128)(2,1)S(1)} %fusion.59), channel_id=1, replica_groups=mesh['dp'=16,'mp'=2] {'mp'}, dimensions={0}, use_global_device_ids=true | all-gather | bytes 663552 | tf_op jit(solution)/shard_map/all_gather | solution.py:115
  347.3 1.4 fusion.93
  (119 shorter events, 4.8 us)
Async XLA Ops:
  7.2 1.3 copy-start
  7.2 23.6 %reduce-scatter.5.cloned.1.call-start = ((), (), s32[]{:S(2)}) async-start(), calls=%async_computation.4 | async-start | bytes 1327104 | tf_op jit(solution)/shard_map/reduce_scatter | solution.py:47
  10.9 129.1 %all-reduce.4.cloned.1.call-start = ((), (), s32[]{:S(2)}) async-start(), calls=%async_computation.3 | async-start | bytes 1769472 | tf_op jit(solution)/shard_map/psum | solution.py:44
  30.8 55.2 %slice-start = ((s8[4958208]{0:T(1024)(128)(4,1)}), s8[4194304]{0:T(1024)(128)(4,1)S(1)}, s32[]{:S(2)}) async-start(s8[4958208]{0:T(1024)(128)(4,1)} %bitcast.18), calls=%async_computation.7 | async-start | bytes 8388608
  33.3 5.4 %collective-permute-start = (bf16[96,1152]{1,0:T(8,128)(2,1)S(1)}, bf16[96,1152]{1,0:T(8,128)(2,1)S(1)}, u32[]{:S(2)}, u32[]{:S(2)}) collective-permute-start(bf16[96,1152]{1,0:T(8,128)(2,1)S(1)} %multiply_convert_fusion.5), channel_id=1, source_target_pairs={{0,2},{2,4},{4,6},{6,8},{8,10},{10,12},{12,14},{14,16},{16,18},{18... | collective-permute-start | bytes 663560 | tf_op jit(solution)/shard_map/ppermute | solution.py:58
  38.7 47.3 %copy-start.5 = (bf16[96,1152]{1,0:T(8,128)(2,1)}, bf16[96,1152]{1,0:T(8,128)(2,1)S(1)}, u32[]{:S(2)}) copy-start(bf16[96,1152]{1,0:T(8,128)(2,1)S(1)} %collective-permute-done) | copy-start | bytes 663556
  38.7 5.4 %collective-permute-start.1 = (bf16[96,1152]{1,0:T(8,128)(2,1)S(1)}, bf16[96,1152]{1,0:T(8,128)(2,1)S(1)}, u32[]{:S(2)}, u32[]{:S(2)}) collective-permute-start(bf16[96,1152]{1,0:T(8,128)(2,1)S(1)} %collective-permute-done), channel_id=1, source_target_pairs={{0,2},{2,4},{4,6},{6,8},{8,10},{10,12},{12,14},{14,16},{16,18},{18... | collective-permute-start | bytes 663560 | tf_op jit(solution)/shard_map/ppermute | solution.py:58
  44.1 41.9 %copy-start.7 = (bf16[96,1152]{1,0:T(8,128)(2,1)}, bf16[96,1152]{1,0:T(8,128)(2,1)S(1)}, u32[]{:S(2)}) copy-start(bf16[96,1152]{1,0:T(8,128)(2,1)S(1)} %collective-permute-done.1) | copy-start | bytes 663556
  44.1 5.4 %collective-permute-start.2 = (bf16[96,1152]{1,0:T(8,128)(2,1)S(1)}, bf16[96,1152]{1,0:T(8,128)(2,1)S(1)}, u32[]{:S(2)}, u32[]{:S(2)}) collective-permute-start(bf16[96,1152]{1,0:T(8,128)(2,1)S(1)} %collective-permute-done.1), channel_id=1, source_target_pairs={{0,2},{2,4},{4,6},{6,8},{8,10},{10,12},{12,14},{14,16},{16,18},{18... | collective-permute-start | bytes 663560 | tf_op jit(solution)/shard_map/ppermute | solution.py:58
  49.4 0.7 copy-start.9
  50.1 5.4 %collective-permute-start.3 = (bf16[96,1152]{1,0:T(8,128)(2,1)S(1)}, bf16[96,1152]{1,0:T(8,128)(2,1)S(1)}, u32[]{:S(2)}, u32[]{:S(2)}) collective-permute-start(bf16[96,1152]{1,0:T(8,128)(2,1)S(1)} %collective-permute-done.2), channel_id=1, source_target_pairs={{0,2},{2,4},{4,6},{6,8},{8,10},{10,12},{12,14},{14,16},{16,18},{18... | collective-permute-start | bytes 663560 | tf_op jit(solution)/shard_map/ppermute | solution.py:58
  55.5 0.7 copy-start.11
  56.2 5.4 %collective-permute-start.4 = (bf16[96,1152]{1,0:T(8,128)(2,1)S(1)}, bf16[96,1152]{1,0:T(8,128)(2,1)S(1)}, u32[]{:S(2)}, u32[]{:S(2)}) collective-permute-start(bf16[96,1152]{1,0:T(8,128)(2,1)S(1)} %collective-permute-done.3), channel_id=1, source_target_pairs={{0,2},{2,4},{4,6},{6,8},{8,10},{10,12},{12,14},{14,16},{16,18},{18... | collective-permute-start | bytes 663560 | tf_op jit(solution)/shard_map/ppermute | solution.py:58
  61.5 0.7 copy-start.13
  62.2 5.4 %collective-permute-start.5 = (bf16[96,1152]{1,0:T(8,128)(2,1)S(1)}, bf16[96,1152]{1,0:T(8,128)(2,1)S(1)}, u32[]{:S(2)}, u32[]{:S(2)}) collective-permute-start(bf16[96,1152]{1,0:T(8,128)(2,1)S(1)} %collective-permute-done.4), channel_id=1, source_target_pairs={{0,2},{2,4},{4,6},{6,8},{8,10},{10,12},{12,14},{14,16},{16,18},{18... | collective-permute-start | bytes 663560 | tf_op jit(solution)/shard_map/ppermute | solution.py:58
  67.6 0.7 copy-start.15
  68.3 5.4 %collective-permute-start.6 = (bf16[96,1152]{1,0:T(8,128)(2,1)S(1)}, bf16[96,1152]{1,0:T(8,128)(2,1)S(1)}, u32[]{:S(2)}, u32[]{:S(2)}) collective-permute-start(bf16[96,1152]{1,0:T(8,128)(2,1)S(1)} %collective-permute-done.5), channel_id=1, source_target_pairs={{0,2},{2,4},{4,6},{6,8},{8,10},{10,12},{12,14},{14,16},{16,18},{18... | collective-permute-start | bytes 663560 | tf_op jit(solution)/shard_map/ppermute | solution.py:58
  71.9 14.1 %slice-start.1 = ((s8[4958208]{0:T(1024)(128)(4,1)}), s8[763904]{0:T(1024)(128)(4,1)S(1)}, s32[]{:S(2)}) async-start(s8[4958208]{0:T(1024)(128)(4,1)} %bitcast.18), calls=%async_computation.8 | async-start | bytes 1527808
  73.7 12.3 %copy-start.17 = (bf16[96,1152]{1,0:T(8,128)(2,1)}, bf16[96,1152]{1,0:T(8,128)(2,1)S(1)}, u32[]{:S(2)}) copy-start(bf16[96,1152]{1,0:T(8,128)(2,1)S(1)} %collective-permute-done.6) | copy-start | bytes 663556
  73.7 8.9 %collective-permute-start.7 = (bf16[96,1152]{1,0:T(8,128)(2,1)S(1)}, bf16[96,1152]{1,0:T(8,128)(2,1)S(1)}, u32[]{:S(2)}, u32[]{:S(2)}) collective-permute-start(bf16[96,1152]{1,0:T(8,128)(2,1)S(1)} %collective-permute-done.6), channel_id=1, source_target_pairs={{0,2},{2,4},{4,6},{6,8},{8,10},{10,12},{12,14},{14,16},{16,18},{18... | collective-permute-start | bytes 663560 | tf_op jit(solution)/shard_map/ppermute | solution.py:58
  82.5 3.5 copy-start.34
  82.5 57.5 %copy-start.2 = (bf16[192,1152]{1,0:T(8,128)(2,1)S(1)}, bf16[192,1152]{1,0:T(8,128)(2,1)}, u32[]{:S(2)}) copy-start(bf16[192,1152]{1,0:T(8,128)(2,1)} %param.8) | copy-start | bytes 1327108
  82.5 64.4 %copy-start.19 = (bf16[96,1152]{1,0:T(8,128)(2,1)}, bf16[96,1152]{1,0:T(8,128)(2,1)S(1)}, u32[]{:S(2)}) copy-start(bf16[96,1152]{1,0:T(8,128)(2,1)S(1)} %collective-permute-done.7) | copy-start | bytes 663556
  82.6 5.9 %collective-permute-start.8 = (bf16[96,1152]{1,0:T(8,128)(2,1)S(1)}, bf16[96,1152]{1,0:T(8,128)(2,1)S(1)}, u32[]{:S(2)}, u32[]{:S(2)}) collective-permute-start(bf16[96,1152]{1,0:T(8,128)(2,1)S(1)} %collective-permute-done.7), channel_id=1, source_target_pairs={{0,2},{2,4},{4,6},{6,8},{8,10},{10,12},{12,14},{14,16},{16,18},{18... | collective-permute-start | bytes 663560 | tf_op jit(solution)/shard_map/ppermute | solution.py:58
  88.5 73.7 %copy-start.1 = (f32[96,1152]{1,0:T(8,128)S(1)}, f32[96,1152]{1,0:T(8,128)}, u32[]{:S(2)}) copy-start(f32[96,1152]{1,0:T(8,128)} %reduce-scatter.5.cloned.1.call-done) | copy-start | bytes 1327108
  88.5 58.4 %copy-start.21 = (bf16[96,1152]{1,0:T(8,128)(2,1)}, bf16[96,1152]{1,0:T(8,128)(2,1)S(1)}, u32[]{:S(2)}) copy-start(bf16[96,1152]{1,0:T(8,128)(2,1)S(1)} %collective-permute-done.8) | copy-start | bytes 663556
  88.5 5.4 %collective-permute-start.9 = (bf16[96,1152]{1,0:T(8,128)(2,1)S(1)}, bf16[96,1152]{1,0:T(8,128)(2,1)S(1)}, u32[]{:S(2)}, u32[]{:S(2)}) collective-permute-start(bf16[96,1152]{1,0:T(8,128)(2,1)S(1)} %collective-permute-done.8), channel_id=1, source_target_pairs={{0,2},{2,4},{4,6},{6,8},{8,10},{10,12},{12,14},{14,16},{16,18},{18... | collective-permute-start | bytes 663560 | tf_op jit(solution)/shard_map/ppermute | solution.py:58
  93.9 53.0 %copy-start.23 = (bf16[96,1152]{1,0:T(8,128)(2,1)}, bf16[96,1152]{1,0:T(8,128)(2,1)S(1)}, u32[]{:S(2)}) copy-start(bf16[96,1152]{1,0:T(8,128)(2,1)S(1)} %collective-permute-done.9) | copy-start | bytes 663556
  93.9 5.4 %collective-permute-start.10 = (bf16[96,1152]{1,0:T(8,128)(2,1)S(1)}, bf16[96,1152]{1,0:T(8,128)(2,1)S(1)}, u32[]{:S(2)}, u32[]{:S(2)}) collective-permute-start(bf16[96,1152]{1,0:T(8,128)(2,1)S(1)} %collective-permute-done.9), channel_id=1, source_target_pairs={{0,2},{2,4},{4,6},{6,8},{8,10},{10,12},{12,14},{14,16},{16,18},{18... | collective-permute-start | bytes 663560 | tf_op jit(solution)/shard_map/ppermute | solution.py:58
  99.3 47.6 %copy-start.25 = (bf16[96,1152]{1,0:T(8,128)(2,1)}, bf16[96,1152]{1,0:T(8,128)(2,1)S(1)}, u32[]{:S(2)}) copy-start(bf16[96,1152]{1,0:T(8,128)(2,1)S(1)} %collective-permute-done.10) | copy-start | bytes 663556
  99.3 5.4 %collective-permute-start.11 = (bf16[96,1152]{1,0:T(8,128)(2,1)S(1)}, bf16[96,1152]{1,0:T(8,128)(2,1)S(1)}, u32[]{:S(2)}, u32[]{:S(2)}) collective-permute-start(bf16[96,1152]{1,0:T(8,128)(2,1)S(1)} %collective-permute-done.10), channel_id=1, source_target_pairs={{0,2},{2,4},{4,6},{6,8},{8,10},{10,12},{12,14},{14,16},{16,18},{18... | collective-permute-start | bytes 663560 | tf_op jit(solution)/shard_map/ppermute | solution.py:58
  104.6 42.3 %copy-start.27 = (bf16[96,1152]{1,0:T(8,128)(2,1)}, bf16[96,1152]{1,0:T(8,128)(2,1)S(1)}, u32[]{:S(2)}) copy-start(bf16[96,1152]{1,0:T(8,128)(2,1)S(1)} %collective-permute-done.11) | copy-start | bytes 663556
  104.6 36.8 %collective-permute-start.12 = (bf16[96,1152]{1,0:T(8,128)(2,1)S(1)}, bf16[96,1152]{1,0:T(8,128)(2,1)S(1)}, u32[]{:S(2)}, u32[]{:S(2)}) collective-permute-start(bf16[96,1152]{1,0:T(8,128)(2,1)S(1)} %collective-permute-done.11), channel_id=1, source_target_pairs={{0,2},{2,4},{4,6},{6,8},{8,10},{10,12},{12,14},{14,16},{16,18},{18... | collective-permute-start | bytes 663560 | tf_op jit(solution)/shard_map/ppermute | solution.py:58
  140.0 18.2 %copy-start.18 = (bf16[96,1152]{1,0:T(8,128)(2,1)S(1)}, bf16[96,1152]{1,0:T(8,128)(2,1)}, u32[]{:S(2)}) copy-start(bf16[96,1152]{1,0:T(8,128)(2,1)} %copy-done.17) | copy-start | bytes 663556
  140.0 22.1 %copy-start.8 = (bf16[96,1152]{1,0:T(8,128)(2,1)S(1)}, bf16[96,1152]{1,0:T(8,128)(2,1)}, u32[]{:S(2)}) copy-start(bf16[96,1152]{1,0:T(8,128)(2,1)} %copy-done.7) | copy-start | bytes 663556
  140.0 22.1 %copy-start.6 = (bf16[96,1152]{1,0:T(8,128)(2,1)S(1)}, bf16[96,1152]{1,0:T(8,128)(2,1)}, u32[]{:S(2)}) copy-start(bf16[96,1152]{1,0:T(8,128)(2,1)} %copy-done.5) | copy-start | bytes 663556
  141.5 21.2 %copy-start.16 = (bf16[96,1152]{1,0:T(8,128)(2,1)S(1)}, bf16[96,1152]{1,0:T(8,128)(2,1)}, u32[]{:S(2)}) copy-start(bf16[96,1152]{1,0:T(8,128)(2,1)} %copy-done.15) | copy-start | bytes 663556
  141.5 5.5 %copy-start.29 = (bf16[96,1152]{1,0:T(8,128)(2,1)}, bf16[96,1152]{1,0:T(8,128)(2,1)S(1)}, u32[]{:S(2)}) copy-start(bf16[96,1152]{1,0:T(8,128)(2,1)S(1)} %collective-permute-done.12) | copy-start | bytes 663556
  141.5 5.4 %collective-permute-start.13 = (bf16[96,1152]{1,0:T(8,128)(2,1)S(1)}, bf16[96,1152]{1,0:T(8,128)(2,1)S(1)}, u32[]{:S(2)}, u32[]{:S(2)}) collective-permute-start(bf16[96,1152]{1,0:T(8,128)(2,1)S(1)} %collective-permute-done.12), channel_id=1, source_target_pairs={{0,2},{2,4},{4,6},{6,8},{8,10},{10,12},{12,14},{14,16},{16,18},{18... | collective-permute-start | bytes 663560 | tf_op jit(solution)/shard_map/ppermute | solution.py:58
  141.6 21.1 %copy-start.14 = (bf16[96,1152]{1,0:T(8,128)(2,1)S(1)}, bf16[96,1152]{1,0:T(8,128)(2,1)}, u32[]{:S(2)}) copy-start(bf16[96,1152]{1,0:T(8,128)(2,1)} %copy-done.13) | copy-start | bytes 663556
  141.6 21.1 %copy-start.12 = (bf16[96,1152]{1,0:T(8,128)(2,1)S(1)}, bf16[96,1152]{1,0:T(8,128)(2,1)}, u32[]{:S(2)}) copy-start(bf16[96,1152]{1,0:T(8,128)(2,1)} %copy-done.11) | copy-start | bytes 663556
  141.6 21.2 %copy-start.10 = (bf16[96,1152]{1,0:T(8,128)(2,1)S(1)}, bf16[96,1152]{1,0:T(8,128)(2,1)}, u32[]{:S(2)}) copy-start(bf16[96,1152]{1,0:T(8,128)(2,1)} %copy-done.9) | copy-start | bytes 663556
  146.9 5.4 %collective-permute-start.14 = (bf16[96,1152]{1,0:T(8,128)(2,1)S(1)}, bf16[96,1152]{1,0:T(8,128)(2,1)S(1)}, u32[]{:S(2)}, u32[]{:S(2)}) collective-permute-start(bf16[96,1152]{1,0:T(8,128)(2,1)S(1)} %collective-permute-done.13), channel_id=1, source_target_pairs={{0,2},{2,4},{4,6},{6,8},{8,10},{10,12},{12,14},{14,16},{16,18},{18... | collective-permute-start | bytes 663560 | tf_op jit(solution)/shard_map/ppermute | solution.py:58
  147.0 15.4 %copy-start.30 = (bf16[96,1152]{1,0:T(8,128)(2,1)S(1)}, bf16[96,1152]{1,0:T(8,128)(2,1)}, u32[]{:S(2)}) copy-start(bf16[96,1152]{1,0:T(8,128)(2,1)} %copy-done.29) | copy-start | bytes 663556
  147.0 15.4 %copy-start.28 = (bf16[96,1152]{1,0:T(8,128)(2,1)S(1)}, bf16[96,1152]{1,0:T(8,128)(2,1)}, u32[]{:S(2)}) copy-start(bf16[96,1152]{1,0:T(8,128)(2,1)} %copy-done.27) | copy-start | bytes 663556
  147.0 15.4 %copy-start.26 = (bf16[96,1152]{1,0:T(8,128)(2,1)S(1)}, bf16[96,1152]{1,0:T(8,128)(2,1)}, u32[]{:S(2)}) copy-start(bf16[96,1152]{1,0:T(8,128)(2,1)} %copy-done.25) | copy-start | bytes 663556
  147.0 15.4 %copy-start.24 = (bf16[96,1152]{1,0:T(8,128)(2,1)S(1)}, bf16[96,1152]{1,0:T(8,128)(2,1)}, u32[]{:S(2)}) copy-start(bf16[96,1152]{1,0:T(8,128)(2,1)} %copy-done.23) | copy-start | bytes 663556
  147.1 15.5 %copy-start.22 = (bf16[96,1152]{1,0:T(8,128)(2,1)S(1)}, bf16[96,1152]{1,0:T(8,128)(2,1)}, u32[]{:S(2)}) copy-start(bf16[96,1152]{1,0:T(8,128)(2,1)} %copy-done.21) | copy-start | bytes 663556
  147.1 15.5 %copy-start.20 = (bf16[96,1152]{1,0:T(8,128)(2,1)S(1)}, bf16[96,1152]{1,0:T(8,128)(2,1)}, u32[]{:S(2)}) copy-start(bf16[96,1152]{1,0:T(8,128)(2,1)} %copy-done.19) | copy-start | bytes 663556
  152.4 10.6 %copy-start.31 = (s32[1536]{0:T(1024)S(1)}, s32[1536]{0:T(1024)}, u32[]{:S(2)}) copy-start(s32[1536]{0:T(1024)} %fusion.76) | copy-start | bytes 18436
  152.4 10.6 %copy-start.33 = (s32[192]{0:T(256)S(1)}, s32[192]{0:T(256)}, u32[]{:S(2)}) copy-start(s32[192]{0:T(256)} %iota_add_fusion) | copy-start | bytes 2308
  163.0 2.8 copy-start.4
  165.8 0.8 copy-start.3
  170.8 164.4 %all-to-all-start = ((f32[16,96,1152]{2,1,0:T(8,128)}), f32[16,96,1152]{2,1,0:T(8,128)}, u32[]{:S(2)}, u32[]{:S(2)}) async-start(f32[16,96,1152]{2,1,0:T(8,128)} %bitcast.16), calls=%async_computation.1 | async-start | bytes 14155776 | tf_op jit(solution)/shard_map/all_to_all | solution.py:85
  181.2 41.1 %all-reduce.6.cloned.1.call-start = ((), (), s32[]{:S(2)}) async-start(), calls=%async_computation.5 | async-start | bytes 1769472 | tf_op jit(solution)/shard_map/psum | solution.py:87
  185.5 71.8 %reduce-scatter.7.cloned.1.call-start = ((), (), s32[]{:S(2)}) async-start(), calls=%async_computation.6 | async-start | bytes 1769472
  226.0 9.4 %copy-start.32 = (f32[1152]{0:T(1024)S(1)}, f32[1152]{0:T(1024)}, u32[]{:S(2)}) copy-start(f32[1152]{0:T(1024)} %param.10) | copy-start | bytes 13828
Sparse Core Ops, SparseCore 0:
  11.1 19.6 reduce-scatter.4
  88.6 51.3 all-reduce.3
  185.7 36.5 all-reduce.5
  235.5 21.8 reduce-scatter.6
